TPU v7x, 8 devices: a whole 2x2x1 slice. The times are simulated.
8 devices in a mesh: ez: 2 (over z, y), ey: 2 (over x), ex: 2 (over core).
Axes of the slice: x: 2, y: 2, z: 1, core: 2. Of those that a mesh axis runs over, the one named last changes fastest.
Arguments:
- tokens: bfloat16 [2048, 1024], P(('ez', 'ey', 'ex'))
- expert_ids: int32 [2048, 8], P(('ez', 'ey', 'ex'))
- gate_weights: float32 [2048, 8], P(('ez', 'ey', 'ex'))
- w_gate: bfloat16 [32, 1024, 512], P(('ez', 'ey', 'ex'))
- w_up: bfloat16 [32, 1024, 512], P(('ez', 'ey', 'ex'))
- w_down: bfloat16 [32, 512, 1024], P(('ez', 'ey', 'ex'))
Outputs:
- output: bfloat16 [2048, 1024], P(('ez', 'ey', 'ex'))
All inputs are finite; a program needn't handle non-finite values.
Results may differ from a plain program's by a relative error of at most 0.00588897.
Values are sent between devices in bfloat16 or wider.
A program may use at most 1 GiB of HBM per device.

v0:
```python
import math
import jax
import jax.numpy as jnp
from jax import lax
from jax.sharding import PartitionSpec as P


def pack_rows(chosen, gate_vals, per_expert):
    row_rank = jnp.cumsum(chosen.astype(jnp.int32), axis=0) - 1
    slot_idx = jnp.where(chosen, row_rank, per_expert)
    row_idx = jnp.broadcast_to(jnp.arange(chosen.shape[0])[:, None], chosen.shape)
    exp_idx = jnp.broadcast_to(jnp.arange(chosen.shape[1])[None, :], chosen.shape)
    pick_rows = jnp.zeros((chosen.shape[1], per_expert), jnp.int32).at[exp_idx, slot_idx].set(row_idx, mode="drop")
    pick_gates = jnp.zeros((chosen.shape[1], per_expert), jnp.float32).at[exp_idx, slot_idx].set(gate_vals, mode="drop")
    return pick_rows, pick_gates


def expert_ffn(x_pack, w_gate, w_up, w_down, pick_gates):
    gate_act = jnp.einsum("lch,lhf->lcf", x_pack, w_gate, preferred_element_type=jnp.float32)
    up_act = jnp.einsum("lch,lhf->lcf", x_pack, w_up, preferred_element_type=jnp.float32)
    hidden_act = (jax.nn.silu(gate_act) * up_act).astype(jnp.bfloat16)
    expert_out = jnp.einsum("lcf,lfh->lch", hidden_act, w_down, preferred_element_type=jnp.float32)
    return expert_out * pick_gates[:, :, None]


def solution(mesh):
    ep_axes = tuple(mesh.axis_names)
    num_devices = math.prod(mesh.shape[axis_name] for axis_name in ep_axes)
    row_spec = P(ep_axes, None)
    w_spec = P(ep_axes, None, None)

    def local_layer(tokens, expert_ids, gate_weights, w_gate, w_up, w_down):
        tok_dev, hidden = tokens.shape
        top_k = expert_ids.shape[1]
        local_experts = w_gate.shape[0]
        capacity = tok_dev * top_k // num_devices
        rows_recv = num_devices * capacity
        per_expert = rows_recv // local_experts
        dest_dev = expert_ids // local_experts
        dev_hit = jnp.any(dest_dev[:, :, None] == jnp.arange(num_devices)[None, None, :], axis=1)
        all_experts = jnp.arange(num_devices * local_experts)
        gate_dense = jnp.sum(jnp.where(expert_ids[:, :, None] == all_experts[None, None, :], gate_weights[:, :, None], 0.0), axis=1)
        gate_dense = gate_dense.reshape(tok_dev, num_devices, local_experts)
        slot_pos = jnp.cumsum(dev_hit.astype(jnp.int32), axis=0) - 1
        place_mask = dev_hit[:, :, None] & (slot_pos[:, :, None] == jnp.arange(capacity)[None, None, :])
        place_bf = place_mask.astype(jnp.bfloat16)
        send_rows = jnp.einsum("tdc,th->dch", place_bf, tokens, preferred_element_type=jnp.float32).astype(jnp.bfloat16)
        send_gates = jnp.sum(jnp.where(place_mask[:, :, :, None], gate_dense[:, :, None, :], 0.0), axis=0)
        recv_rows = lax.all_to_all(send_rows, ep_axes, 0, 0, tiled=True)
        recv_gates = lax.all_to_all(send_gates, ep_axes, 0, 0, tiled=True)
        flat_rows = recv_rows.reshape(rows_recv, hidden)
        flat_gates = recv_gates.reshape(rows_recv, local_experts)
        pick_rows, pick_gates = pack_rows(flat_gates > 0.0, flat_gates, per_expert)
        weighted = expert_ffn(flat_rows[pick_rows], w_gate, w_up, w_down, pick_gates)
        part_sum = jax.ops.segment_sum(weighted.reshape(-1, hidden), pick_rows.reshape(-1), num_segments=rows_recv)
        back_rows = part_sum.astype(jnp.bfloat16).reshape(num_devices, capacity, hidden)
        returned = lax.all_to_all(back_rows, ep_axes, 0, 0, tiled=True)
        moe_sum = jnp.einsum("tdc,dch->th", place_bf, returned, preferred_element_type=jnp.float32)
        return (tokens.astype(jnp.float32) + moe_sum).astype(jnp.bfloat16)

    return jax.shard_map(local_layer, mesh=mesh, in_specs=(row_spec, row_spec, row_spec, w_spec, w_spec, w_spec), out_specs=row_spec, check_vma=False)
```

profile of v0, /device:TPU:0, one launch (start us, length us, event | category | flops | bytes accessed | tf_op | source)
XLA Modules:
  0.0 200.6 jit_solution(750366226276056847)
XLA Ops:
  0.0 0.7 add_select_fusion
  0.7 0.6 reduce-window.14
  1.3 0.2 slice_reduce_fusion.1
  1.6 0.1 add_bitcast_fusion.1
  1.7 0.8 select_reduce_fusion.1
  2.4 0.2 copy.29
  2.7 0.7 fusion.2
  3.4 0.5 copy.28
  3.9 1.8 select_reduce_fusion
  5.7 0.6 copy.30
  6.4 4.3 %all-to-all-start = ((f32[8,256,4]{1,2,0:T(4,128)}), f32[8,256,4]{1,2,0:T(4,128)S(1)}, u32[]{:S(2)}, u32[]{:S(2)}) async-start(f32[8,256,4]{1,2,0:T(4,128)} %copy.30), calls=%async_computation | async-start | bytes 65536 | tf_op jit(solution)/shard_map/all_to_all | solution.py:50
  10.7 4.5 %convolution_convert_fusion = bf16[8,256,1024]{2,1,0:T(8,128)(2,1)} fusion(bf16[256,1024]{1,0:T(8,128)(2,1)} %param.6, s32[256,8]{0,1:T(8,128)S(1)} %add_bitcast_fusion.1, pred[256,8]{0,1:T(8,128)(4,1)S(1)} %fusion.6), kind=kOutput, calls=%fused_computation.9 | convolution fusion | flops 1076887552 | bytes 4728832 | tf_op jit(solution)/shard_map/tdc,th->dch/dot_general | solution.py:47
  15.2 0.0 copy-start.2
  15.2 0.0 copy-start.1
  15.2 0.1 all-to-all-done
  15.3 3.3 %all-to-all-start.1 = ((bf16[8,256,1024]{2,1,0:T(8,128)(2,1)}), bf16[8,256,1024]{2,1,0:T(8,128)(2,1)}, u32[]{:S(2)}, u32[]{:S(2)}) async-start(bf16[8,256,1024]{2,1,0:T(8,128)(2,1)} %convolution_convert_fusion), calls=%async_computation.1 | async-start | bytes 8388608 | tf_op jit(solution)/shard_map/all_to_all | solution.py:49
  18.6 0.1 broadcast_in_dim.85
  18.7 0.6 reshape.96
  19.4 1.2 reduce-window.16
  20.5 0.2 slice_reduce_fusion
  20.7 0.2 reduce-window.19
  20.9 0.1 add_bitcast_fusion
  21.1 0.0 copy-done.2
  21.1 0.1 multiply_reduce_fusion
  21.2 0.0 copy-done.1
  21.2 0.1 and_reduce_fusion
  21.3 0.4 copy.31
  21.7 0.6 reshape.94
  22.3 0.4 copy.33
  22.7 0.6 reshape.102
  23.3 30.4 %scatter_custom_fusion.2 = f32[2048]{0:T(1024)S(1)} fusion(s32[8192]{0:T(1024)S(1)} %reshape.94, f32[8192]{0:T(1024)S(1)} %reshape.102, f32[]{:T(128)} %constant.41.clone.1), kind=kCustom, calls=%fused_computation.46 | custom fusion | bytes 8196
  53.8 30.6 %scatter_custom_fusion.1 = s32[2048]{0:T(1024)S(1)} fusion(s32[8192]{0:T(1024)S(1)} %reshape.94, s32[8192]{0:T(1024)S(1)} %reshape.96, s32[]{:T(128)} %constant.20.clone.1), kind=kCustom, calls=%fused_computation.48 | custom fusion | bytes 8196 | tf_op jit(solution)/shard_map/broadcast_in_dim;reshape | solution.py:55
  84.5 0.0 all-to-all-done.1
  84.5 13.7 %gather_fusion = bf16[2048,1024]{1,0:T(8,128)(2,1)} fusion(bf16[2048,1024]{1,0:T(8,128)(2,1)} %bitcast.9, s32[2048]{0:T(1024)S(1)} %broadcast_clamp_fusion), kind=kCustom, calls=%fused_computation | custom fusion | bytes 8396800 | tf_op jit(solution)/shard_map/gather | solution.py:54
  98.2 7.8 %fusion.19 = f32[4,512,512]{2,1,0:T(8,128)} fusion(bf16[4,512,1024]{2,1,0:T(8,128)(2,1)} %bitcast.59, bf16[4,1024,512]{2,1,0:T(8,128)(2,1)} %param.9), kind=kOutput, calls=%fused_computation.51 | convolution fusion | flops 2147483648 | bytes 12582912 | tf_op jit(solution)/shard_map/lch,lhf->lcf/dot_general | solution.py:19
  106.0 13.7 %broadcast_multiply_fusion = f32[4,512,1024]{2,1,0:T(8,128)} fusion(f32[4,512]{1,0:T(4,128)S(1)} %reshape.74, bf16[4,512,1024]{2,1,0:T(8,128)(2,1)} %param.11, f32[4,512,512]{2,1,0:T(8,128)} %fusion.19, bf16[4,512,1024]{2,1,0:T(8,128)(2,1)} %bitcast.60, bf16[4,1024,512]{2,1,0:T(8,128)(2,1)} %param.10), kind=kOutput, calls=%fused_computation.5 | convolution fusion | flops 4303355904 | bytes 25174016 | tf_op jit(solution)/shard_map/lcf,lfh->lch/dot_general | solution.py:22
  119.7 22.7 %scatter_custom_fusion = f32[2048,1024]{1,0:T(8,128)} fusion(s32[2048]{0:T(1024)S(1)} %scatter_custom_fusion.1, f32[2048,1024]{1,0:T(8,128)} %bitcast.66, f32[]{:T(128)} %constant.41.clone.1), kind=kCustom, calls=%fused_computation.7 | custom fusion | flops 2097152 | bytes 8389120 | tf_op jit(solution)/shard_map/scatter-add | solution.py:55
  142.4 4.0 %convert_element_type.26 = bf16[2048,1024]{1,0:T(8,128)(2,1)S(1)} convert(f32[2048,1024]{1,0:T(8,128)} %scatter_custom_fusion) | non-fusion elementwise | flops 2097152 | bytes 12582912 | tf_op jit(solution)/shard_map/convert_element_type | solution.py:56
  146.4 0.0 copy-start
  146.4 51.7 %all_to_all.15 = bf16[8,256,1024]{2,1,0:T(8,128)(2,1)S(1)} all-to-all(bf16[8,256,1024]{2,1,0:T(8,128)(2,1)S(1)} %bitcast.58), channel_id=1, replica_groups=mesh['ez'=2,'ey'=2,'ex'=2] {'ez','ey','ex'}, dimensions={0} | all-to-all | bytes 8388608 | tf_op jit(solution)/shard_map/all_to_all | solution.py:57
  198.2 0.0 copy-done
  198.2 2.4 %fusion.4 = bf16[256,1024]{1,0:T(8,128)(2,1)} fusion(bf16[8,256,1024]{2,1,0:T(8,128)(2,1)S(1)} %all_to_all.15, bf16[256,1024]{1,0:T(8,128)(2,1)S(1)} %copy-done, s32[256,8]{0,1:T(8,128)S(1)} %add_bitcast_fusion.1, pred[256,8]{0,1:T(8,128)(4,1)S(1)} %fusion.6), kind=kOutput, calls=%fused_computation.14 | convolution fusion | flops 1075576832 | bytes 5253120 | tf_op jit(solution)/shard_map/tdc,dch->th/dot_general | solution.py:58
  (16 shorter events, 0.2 us)
Async XLA Ops:
  6.4 8.9 %all-to-all-start = ((f32[8,256,4]{1,2,0:T(4,128)}), f32[8,256,4]{1,2,0:T(4,128)S(1)}, u32[]{:S(2)}, u32[]{:S(2)}) async-start(f32[8,256,4]{1,2,0:T(4,128)} %copy.30), calls=%async_computation | async-start | bytes 65536 | tf_op jit(solution)/shard_map/all_to_all | solution.py:50
  15.2 5.9 %copy-start.2 = (s32[2]{0:T(128)S(1)}, s32[2]{0:T(128)}, u32[]{:S(2)}) copy-start(s32[2]{0:T(128)} %constant.48) | copy-start | bytes 28
  15.2 6.0 %copy-start.1 = (s32[2]{0:T(128)S(1)}, s32[2]{0:T(128)}, u32[]{:S(2)}) copy-start(s32[2]{0:T(128)} %constant.51) | copy-start | bytes 28
  15.3 69.2 %all-to-all-start.1 = ((bf16[8,256,1024]{2,1,0:T(8,128)(2,1)}), bf16[8,256,1024]{2,1,0:T(8,128)(2,1)}, u32[]{:S(2)}, u32[]{:S(2)}) async-start(bf16[8,256,1024]{2,1,0:T(8,128)(2,1)} %convolution_convert_fusion), calls=%async_computation.1 | async-start | bytes 8388608 | tf_op jit(solution)/shard_map/all_to_all | solution.py:49
  146.4 51.7 %copy-start = (bf16[256,1024]{1,0:T(8,128)(2,1)S(1)}, bf16[256,1024]{1,0:T(8,128)(2,1)}, u32[]{:S(2)}) copy-start(bf16[256,1024]{1,0:T(8,128)(2,1)} %param.6) | copy-start | bytes 1572868
where the time goes:
time: 201 us
  local copies, waits for them, and re-layouts  79.4 us (40%)
  blocking collectives  51.7 us (26%)
  other arithmetic  33.2 us (17%)
  matrix products  28.4 us (14%)
  starting transfers between devices  7.58 us (4%)
    all_to_all x1, blocking collectives, local_layer(): returned = lax.all_to_all(back_rows, ep_axes, 0, 0, tiled=True)  51.7 us
    unnamed x11, local copies, waits for them, and re-layouts  31.5 us
    another operation x1, local copies, waits for them, and re-layouts, local_layer(): jax.ops.segment_sum(weighted.reshape(-1, hidden), pick_rows.reshape(-1),...  30.6 us
    scatter-add x1, other arithmetic, local_layer(): jax.ops.segment_sum(weighted.reshape(-1, hidden), pick_rows.reshape(-1),...  22.7 us
    dot_general x1, matrix products, expert_ffn(): jnp.einsum('lcf,lfh->lch', hidden_act, w_down, preferred_element_type=jnp...  13.7 us
    gather x1, local copies, waits for them, and re-layouts, local_layer(): flat_rows[pick_rows]  13.7 us
    dot_general x1, matrix products, expert_ffn(): jnp.einsum('lch,lhf->lcf', x_pack, w_gate, preferred_element_type=jnp.flo...  7.76 us
    dot_general x1, matrix products, local_layer(): jnp.einsum('tdc,th->dch', place_bf, tokens, preferred_element_type=jnp.fl...  4.51 us
  transfers between devices with their start and end apart: 2, of which 1 were waited for; matrix products, arithmetic and copies ran while one was open for 35% of the time, Pallas kernels for 0%

commit v1 on v0

v1 whole, which is shorter than its diff:
```python
import functools

import jax
import jax.numpy as jnp
from jax import lax
from jax.experimental import pallas as pl
from jax.experimental.pallas import tpu as pltpu
from jax.sharding import PartitionSpec as P

MESH = pl.DeviceIdType.MESH
F32, BF16 = jnp.float32, jnp.bfloat16

BLOCKS = (
    ((0, 0), (0, 1)),
    ((1, 0), (1, 1)),
    ((3, 0), (5, 1)),
    ((2, 0), (4, 1)),
    ((7, 0), (7, 1)),
    ((6, 0), (6, 1)),
    ((3, 1), (5, 0)),
    ((2, 1), (4, 0)),
)
GATE_ORDER = (0, 1, 4, 5, 2, 3, 6, 7)


def moe_kernel(
    x_hbm, ids_hbm, gates_hbm, w1_hbm, w3_hbm, w2_hbm, y_hbm,
    xs, w1, w3, w2, ids, gates, gsend, g_a, g_b, g_d, g_c, G,
    acc, own, out_c, rec_c, pb, r_a, r_b, d_a, d_b, y_buf, lsem, ssem, rsem,
):
    z, y, x = lax.axis_index("ez"), lax.axis_index("ey"), lax.axis_index("ex")
    me = 4 * z + 2 * y + x
    dev = {"A": (z, 1 - y, x), "B": (1 - z, y, x), "C": (z, y, 1 - x)}
    half = 128
    local_experts, top_k = w1.shape[0], ids.shape[0]
    count = [0, 0]

    def local(src, dst):
        copy = pltpu.make_async_copy(src, dst, lsem.at[count[0]])
        count[0] += 1
        return copy

    def remote(src, dst, to):
        copy = pltpu.make_async_remote_copy(
            src_ref=src, dst_ref=dst, send_sem=ssem.at[count[1]], recv_sem=rsem.at[count[1]],
            device_id=dev[to], device_id_type=MESH,
        )
        count[1] += 1
        sent.append(copy)
        return copy

    sent = []
    lo, hi = pl.ds(0, half), pl.ds(half, half)

    load_ids, load_gates = local(ids_hbm, ids), local(gates_hbm, gates)
    load_x = local(x_hbm, xs.at[0])
    load_ids.start()
    load_gates.start()
    load_x.start()
    load_w = []
    for e in range(local_experts):
        trio = [local(s.at[e], d.at[e]) for s, d in ((w1_hbm, w1), (w3_hbm, w3), (w2_hbm, w2))]
        for copy in trio:
            copy.start()
        load_w.append(trio)

    barrier = pltpu.get_barrier_semaphore()
    for to in "ABC":
        pl.semaphore_signal(barrier, inc=1, device_id=dev[to], device_id_type=MESH)

    load_ids.wait()
    load_gates.wait()
    ids_v, gates_v = ids[...], gates[...]
    for p, k in enumerate(GATE_ORDER):
        first = (me ^ k) * local_experts
        for e in range(local_experts):
            row = jnp.sum(jnp.where(ids_v == first + e, gates_v, 0.0), axis=0, keepdims=True)
            gsend[p, pl.ds(2 * e, 1), :] = row[:, :half]
            gsend[p, pl.ds(2 * e + 1, 1), :] = row[:, half:]
    load_x.wait()
    pl.semaphore_wait(barrier, 3)

    quarter = half // 2
    ag_a1 = remote(xs.at[0, lo], xs.at[3, lo], "A")
    ag_b1 = remote(xs.at[0, hi], xs.at[3, hi], "B")
    gs_a = remote(gsend.at[pl.ds(4, 4)], g_a, "A")
    gs_b = remote(gsend.at[pl.ds(2, 2)], g_b, "B")
    ag_c1 = remote(xs.at[0], xs.at[1], "C")
    gs_c = remote(gsend.at[pl.ds(1, 1)], g_c.at[pl.ds(0, 1)], "C")
    ag_a2 = [remote(xs.at[0, pl.ds(half + q * quarter, quarter)], xs.at[7, pl.ds(q * quarter, quarter)], "A") for q in range(2)]
    ag_b2 = [remote(xs.at[0, pl.ds(q * quarter, quarter)], xs.at[7, pl.ds(half + q * quarter, quarter)], "B") for q in range(2)]
    fw_a = remote(xs.at[3, hi], xs.at[5, hi], "A")
    fw_b = remote(xs.at[3, lo], xs.at[5, lo], "B")
    gf_b = remote(g_a.at[pl.ds(2, 2)], g_d, "B")
    d2d_3 = remote(xs.at[3], xs.at[2], "C")
    d2d_5 = remote(xs.at[5], xs.at[4], "C")
    d2d_7 = remote(xs.at[7], xs.at[6], "C")
    gc_3 = remote(g_a.at[pl.ds(1, 1)], g_c.at[pl.ds(1, 1)], "C")
    gc_5 = remote(g_b.at[pl.ds(1, 1)], g_c.at[pl.ds(2, 1)], "C")
    gc_7 = remote(g_d.at[pl.ds(1, 1)], g_c.at[pl.ds(3, 1)], "C")

    for copy in (ag_a1, ag_b1, ag_c1, gs_c, gs_a, gs_b, ag_a2[0], ag_b2[0]):
        copy.start()

    def forward_3():
        ag_a1.wait_recv()
        ag_b1.wait_recv()
        gs_a.wait_recv()
        gs_b.wait_recv()
        for copy in (fw_a, fw_b, gf_b, d2d_3, gc_3, gc_5, ag_a2[1], ag_b2[1]):
            copy.start()

    def forward_5():
        fw_a.wait_recv()
        fw_b.wait_recv()
        gf_b.wait_recv()
        d2d_5.start()
        gc_7.start()

    def forward_7():
        for copy in ag_a2 + ag_b2:
            copy.wait_recv()
        d2d_7.start()

    def gate_tile(owner):
        return {
            0: gsend.at[0], 1: g_c.at[0], 2: g_a.at[0], 3: g_c.at[1],
            4: g_b.at[0], 5: g_c.at[2], 6: g_d.at[0], 7: g_c.at[3],
        }[owner]

    def hidden(s, e):
        rows = xs[s]
        mask = jnp.concatenate([G[e]] * (w1.shape[2] // 128), axis=1) > 0.0
        a = jnp.dot(rows, w1[e], preferred_element_type=F32)
        b = jnp.dot(rows, w3[e], preferred_element_type=F32)
        return jnp.where(mask, a * (1.0 / (1.0 + jnp.exp(-a))) * b, 0.0).astype(BF16)

    def experts(s, total, hooks=None):
        hooks = hooks or {}
        for e in range(local_experts):
            for i, (owner, h) in enumerate(BLOCKS[s]):
                row = gate_tile(owner)[pl.ds(2 * e + h, 1), :]
                G[e, pl.ds(i * half, half), :] = jnp.broadcast_to(row, (half, half)).T
        act = None
        for e in range(local_experts + 1):
            if e in hooks:
                hooks[e]()
            later = hidden(s, e) if e < local_experts else None
            if act is not None:
                out = jnp.dot(act, w2[e - 1], preferred_element_type=F32)
                out = out * jnp.concatenate([G[e - 1]] * (w2.shape[2] // 128), axis=1)
                if e == 1:
                    total[...] = out
                else:
                    total[...] += out
            act = later

    def wait_weights(e):
        for copy in load_w[e]:
            copy.wait()

    experts(0, own, {e: functools.partial(wait_weights, e) for e in range(local_experts)})
    ag_c1.wait_recv()
    gs_c.wait_recv()
    experts(1, acc, {3: forward_3})
    out_c[0] = acc[...].astype(BF16)
    rs_c = [remote(out_c.at[i], rec_c.at[i], "C") for i in range(4)]
    rs_c[0].start()

    d2d_3.wait_recv()
    gc_3.wait_recv()
    gc_5.wait_recv()
    experts(2, acc)
    out_c[1] = acc[...].astype(BF16)
    rs_c[1].start()
    experts(3, acc, {3: forward_5})
    rs_c[1].wait_recv()
    pb[0] = (acc[...] + rec_c[1].astype(F32)).astype(BF16)
    rs_a1 = remote(pb.at[0, lo], r_a.at[lo], "A")
    rs_b1 = remote(pb.at[0, hi], r_b.at[hi], "B")
    rs_a1.start()
    rs_b1.start()

    d2d_5.wait_recv()
    gc_7.wait_recv()
    experts(4, acc)
    out_c[2] = acc[...].astype(BF16)
    rs_c[2].start()
    experts(5, acc, {2: forward_7})
    rs_c[2].wait_recv()
    pb[1] = (acc[...] + rec_c[2].astype(F32)).astype(BF16)
    rs_d = []
    for q in range(2):
        rs_d.append((
            remote(pb.at[1, pl.ds(q * quarter, quarter)], d_a.at[pl.ds(q * quarter, quarter)], "A"),
            remote(pb.at[1, pl.ds(half + q * quarter, quarter)], d_b.at[pl.ds(q * quarter, quarter)], "B"),
        ))
        for copy in rs_d[q]:
            copy.start()

    d2d_7.wait_recv()
    experts(6, acc)
    out_c[3] = acc[...].astype(BF16)
    rs_c[3].start()
    experts(7, acc)
    rs_c[3].wait_recv()
    rs_2 = []
    for q in range(2):
        upper, lower = pl.ds(q * quarter, quarter), pl.ds(half + q * quarter, quarter)
        rs_d[q][1].wait_recv()
        pb[2, upper] = (acc[upper, :] + rec_c[3, upper].astype(F32) + d_b[upper].astype(F32)).astype(BF16)
        rs_2.append([remote(pb.at[2, upper], r_a.at[lower], "A")])
        rs_2[q][0].start()
        rs_d[q][0].wait_recv()
        pb[2, lower] = (acc[lower, :] + rec_c[3, lower].astype(F32) + d_a[upper].astype(F32)).astype(BF16)
        rs_2[q].append(remote(pb.at[2, lower], r_b.at[upper], "B"))
        rs_2[q][1].start()

    rs_c[0].wait_recv()
    rs_a1.wait_recv()
    rs_b1.wait_recv()
    own[...] = own[...] + rec_c[0].astype(F32) + xs[0].astype(F32)
    own[lo, :] = own[lo, :] + r_a[lo].astype(F32)
    own[hi, :] = own[hi, :] + r_b[hi].astype(F32)
    stores = []
    for q in range(2):
        upper, lower = pl.ds(q * quarter, quarter), pl.ds(half + q * quarter, quarter)
        rs_2[q][0].wait_recv()
        y_buf[lower] = (own[lower, :] + r_a[lower].astype(F32)).astype(BF16)
        rs_2[q][1].wait_recv()
        y_buf[upper] = (own[upper, :] + r_b[upper].astype(F32)).astype(BF16)
        for rows in (upper, lower):
            stores.append(local(y_buf.at[rows], y_hbm.at[rows]))
            stores[-1].start()
    for copy in stores:
        copy.wait()
    for copy in sent:
        copy.wait_send()


def solution(mesh):
    axes = tuple(mesh.axis_names)
    row_spec, w_spec = P(axes, None), P(axes, None, None)

    def local_layer(tokens, expert_ids, gate_weights, w_gate, w_up, w_down):
        rows, width = tokens.shape
        experts, _, ff = w_gate.shape
        top_k = expert_ids.shape[1]
        any_space = pl.BlockSpec(memory_space=pl.ANY)
        return pl.pallas_call(
            moe_kernel,
            name="moe_layer",
            out_shape=jax.ShapeDtypeStruct((rows, width), BF16),
            in_specs=[any_space] * 6,
            out_specs=any_space,
            scratch_shapes=[
                pltpu.VMEM((8, rows, width), BF16),
                pltpu.VMEM((experts, width, ff), BF16),
                pltpu.VMEM((experts, width, ff), BF16),
                pltpu.VMEM((experts, ff, width), BF16),
                pltpu.VMEM((top_k, rows), jnp.int32),
                pltpu.VMEM((top_k, rows), F32),
                pltpu.VMEM((8, 8, 128), F32),
                pltpu.VMEM((4, 8, 128), F32),
                pltpu.VMEM((2, 8, 128), F32),
                pltpu.VMEM((2, 8, 128), F32),
                pltpu.VMEM((4, 8, 128), F32),
                pltpu.VMEM((experts, rows, 128), F32),
                pltpu.VMEM((rows, width), F32),
                pltpu.VMEM((rows, width), F32),
                pltpu.VMEM((4, rows, width), BF16),
                pltpu.VMEM((4, rows, width), BF16),
                pltpu.VMEM((3, rows, width), BF16),
                pltpu.VMEM((rows, width), BF16),
                pltpu.VMEM((rows, width), BF16),
                pltpu.VMEM((rows // 2, width), BF16),
                pltpu.VMEM((rows // 2, width), BF16),
                pltpu.VMEM((rows, width), BF16),
                pltpu.SemaphoreType.DMA((20,)),
                pltpu.SemaphoreType.DMA((40,)),
                pltpu.SemaphoreType.DMA((40,)),
            ],
            compiler_params=pltpu.CompilerParams(
                collective_id=0, has_side_effects=True, vmem_limit_bytes=60 * 2**20
            ),
        )(tokens, expert_ids.T, gate_weights.T, w_gate, w_up, w_down)

    return jax.shard_map(
        local_layer, mesh=mesh,
        in_specs=(row_spec, row_spec, row_spec, w_spec, w_spec, w_spec),
        out_specs=row_spec, check_vma=False,
    )
```

time: 201 us -> 48.2 us (0.24)
  local copies, waits for them, and re-layouts: 79.4 us -> 1.87 us
  blocking collectives: 51.7 us -> 0 us
  Pallas kernels: 0 us -> 46.2 us
  other arithmetic: 33.2 us -> 0 us
  matrix products: 28.4 us -> 0 us
  starting transfers between devices: 7.58 us -> 0 us
    all_to_all x1 -> x0, blocking collectives: 51.7 us -> none  [local_layer(): returned = lax.all_to_all(back_rows, ep_axes, 0, 0, tiled=True)]
    pallas_call x0 -> x1, Pallas kernels: none -> 46.2 us  [local_layer(): pl.pallas_call(moe_kernel, name='moe_layer', out_shape=jax.ShapeDtypeStru...]
    another operation x3 -> x0, local copies, waits for them, and re-layouts: 30.8 us -> none  [the longest x1 30.6 us: local_layer(): jax.ops.segment_sum(weighted.reshape(-1, hidden), pick_rows.reshape(-1),...]
    unnamed x11 -> x1, local copies, waits for them, and re-layouts: 31.5 us -> 1.87 us
    dot_general x4 -> x0, matrix products: 28.4 us -> none  [the longest x1 13.7 us: expert_ffn(): jnp.einsum('lcf,lfh->lch', hidden_act, w_down, preferred_element_type=jnp...]
    scatter-add x1 -> x0, other arithmetic: 22.7 us -> none  [local_layer(): jax.ops.segment_sum(weighted.reshape(-1, hidden), pick_rows.reshape(-1),...]
    gather x1 -> x0, local copies, waits for them, and re-layouts: 13.7 us -> none  [local_layer(): flat_rows[pick_rows]]
    all_to_all x2 -> x0, starting transfers between devices: 7.58 us -> none  [the longest x1 4.3 us: local_layer(): recv_gates = lax.all_to_all(send_gates, ep_axes, 0, 0, tiled=True)]
  transfers between devices with their start and end apart: 2 -> 0, of which waited for: 1 -> 0; matrix products, arithmetic and copies ran while one was open for 35% -> 0% of each run, Pallas kernels for 0% -> 0%
where the time goes in v1:
time: 48.2 us; the launch traced here: 48.1 us
  Pallas kernels  46.2 us (96%)
  local copies, waits for them, and re-layouts  1.87 us (4%)
    pallas_call x1, Pallas kernels, local_layer(): pl.pallas_call(moe_kernel, name='moe_layer', out_shape=jax.ShapeDtypeStru...  46.2 us
    unnamed x1, local copies, waits for them, and re-layouts  1.87 us

profile of v1, /device:TPU:0, one launch (start us, length us, event | category | flops | bytes accessed | tf_op | source)
XLA Modules:
  0.0 48.1 jit_solution(9880312837136873275)
XLA Ops:
  0.0 46.2 %moe_layer.1 = bf16[256,1024]{1,0:T(8,128)(2,1)} custom-call(bf16[256,1024]{1,0:T(8,128)(2,1)} %x_hbm.1, s32[8,256]{1,0:T(8,128)} %bitcast.2, f32[8,256]{1,0:T(8,128)} %bitcast.3, bf16[4,1024,512]{2,1,0:T(8,128)(2,1)} %w1_hbm.1, bf16[4,1024,512]{2,1,0:T(8,128)(2,1)} %w3_hbm.1, bf16[4,512,1024]{2,1,0:T(8,128)(2,1)} %w2_hbm.1), custom_call_target="tpu_custom_call" | custom-call | tf_op jit(solution)/shard_map/moe_layer/pallas_call | solution.py:250
  46.2 1.9 %copy.8 = bf16[256,1024]{1,0:T(8,128)(2,1)} copy(bf16[256,1024]{1,0:T(8,128)(2,1)} %moe_layer.1) | data formatting | bytes 1048576

commit v2 on v0

v2 whole, which is shorter than its diff:
```python
import functools

import jax
import jax.numpy as jnp
from jax import lax
from jax.experimental import pallas as pl
from jax.experimental.pallas import tpu as pltpu
from jax.sharding import PartitionSpec as P

MESH = pl.DeviceIdType.MESH
F32, BF16 = jnp.float32, jnp.bfloat16

BLOCKS = (
    ((0, 0, 0), (0, 0, 1), (0, 1, 0), (0, 1, 1)),
    ((1, 0, 0), (1, 0, 1), (1, 1, 0), (1, 1, 1)),
    ((3, 0, 0), (5, 1, 1), (2, 0, 0), (4, 1, 1)),
    ((5, 1, 0), (3, 0, 1), (4, 1, 0), (2, 0, 1)),
    ((7, 0, 0), (7, 1, 1), (6, 0, 0), (6, 1, 1)),
    ((7, 1, 0), (7, 0, 1), (6, 1, 0), (6, 0, 1)),
    ((5, 0, 0), (3, 1, 1), (4, 0, 0), (2, 1, 1)),
    ((3, 1, 0), (5, 0, 1), (2, 1, 0), (4, 0, 1)),
)
GATE_ORDER = (0, 1, 4, 5, 2, 3, 6, 7)
QUARTER = 64


def place(piece):
    for s, pieces in enumerate(BLOCKS):
        if piece in pieces:
            return s, pieces.index(piece) * QUARTER


def token_row(half, quarter):
    return (2 * half + quarter) * QUARTER


def moe_kernel(
    x_hbm, ids_hbm, gates_hbm, w1_hbm, w3_hbm, w2_hbm, y_hbm,
    xs, w1, w3, w2, ids, gates, gsend, g_a, g_b, g_d, g_c, G,
    acc, own, out_c1, rec_c1, out_c, rec_c, pb, r_a, r_b, d_a, d_b, y_buf, lsem, ssem, rsem,
):
    z, y, x = lax.axis_index("ez"), lax.axis_index("ey"), lax.axis_index("ex")
    me = 4 * z + 2 * y + x
    dev = {"A": (z, 1 - y, x), "B": (1 - z, y, x), "C": (z, y, 1 - x)}
    half = 2 * QUARTER
    local_experts = w1.shape[0]
    count = [0, 0]
    sent = []

    def local(src, dst):
        copy = pltpu.make_async_copy(src, dst, lsem.at[count[0]])
        count[0] += 1
        return copy

    def remote(src, dst, to):
        copy = pltpu.make_async_remote_copy(
            src_ref=src, dst_ref=dst, send_sem=ssem.at[count[1]], recv_sem=rsem.at[count[1]],
            device_id=dev[to], device_id_type=MESH,
        )
        count[1] += 1
        sent.append(copy)
        return copy

    def rows(piece, skip=0, size=QUARTER):
        s, row = place(piece)
        return xs.at[s, pl.ds(row + skip, size)]

    def start(copies):
        for copy in copies:
            copy.start()

    def arrive(copies):
        for copy in copies:
            copy.wait_recv()

    load_x = local(x_hbm, xs.at[0])
    load_ids, load_gates = local(ids_hbm, ids), local(gates_hbm, gates)
    start((load_x, load_ids, load_gates))
    load_w = []
    for e in range(local_experts):
        load_w.append([local(s.at[e], d.at[e]) for s, d in ((w1_hbm, w1), (w3_hbm, w3), (w2_hbm, w2))])
        start(load_w[e])
    load_w.append([])

    barrier = pltpu.get_barrier_semaphore()
    for to in "ABC":
        pl.semaphore_signal(barrier, inc=1, device_id=dev[to], device_id_type=MESH)

    first, second, onward = ([], []), ([], []), ([], [])
    for i in range(2):
        s1, s2, s3 = 2 + i, 4 + i, 6 + i
        for owner, h, q in BLOCKS[s1][2:]:
            to, across = ("A", "B") if owner == 2 else ("B", "A")
            first[i].append(remote(rows((0, h, q)), rows((owner, h, q)), to))
            onward[i].append(remote(rows((owner, h, q)), rows((6, h, q)), across))
        for owner, h, q in BLOCKS[s3][2:]:
            to = "A" if owner == 2 else "B"
            cuts = ((0, 32), (32, 32)) if i == 0 else ((0, QUARTER),)
            second[i].append([remote(rows((0, h, q), *cut), rows((owner, h, q), *cut), to) for cut in cuts])
    core_own = remote(xs.at[0], xs.at[1], "C")
    upper, lower = pl.ds(0, half), pl.ds(half, half)
    core = {s: remote(xs.at[s, lower], xs.at[s, upper], "C") for s in range(2, 8)}
    gate_a = remote(gsend.at[pl.ds(4, 4)], g_a, "A")
    gate_b = remote(gsend.at[pl.ds(2, 2)], g_b, "B")
    gate_c = remote(gsend.at[pl.ds(1, 1)], g_c.at[pl.ds(0, 1)], "C")
    gate_d = remote(g_a.at[pl.ds(2, 2)], g_d, "B")
    gate_c3 = remote(g_a.at[pl.ds(1, 1)], g_c.at[pl.ds(1, 1)], "C")
    gate_c5 = remote(g_b.at[pl.ds(1, 1)], g_c.at[pl.ds(2, 1)], "C")
    gate_c7 = remote(g_d.at[pl.ds(1, 1)], g_c.at[pl.ds(3, 1)], "C")

    load_x.wait()
    pl.semaphore_wait(barrier, 3)
    start(first[0])

    load_ids.wait()
    load_gates.wait()
    ids_v, gates_v = ids[...], gates[...]
    for p, k in enumerate(GATE_ORDER):
        base = (me ^ k) * local_experts
        for e in range(local_experts):
            row = jnp.sum(jnp.where(ids_v == base + e, gates_v, 0.0), axis=0, keepdims=True)
            gsend[p, pl.ds(2 * e, 1), :] = row[:, :half]
            gsend[p, pl.ds(2 * e + 1, 1), :] = row[:, half:]
    start((gate_a, gate_b, gate_c, core_own))
    start(first[1])
    start([pieces[0] for pieces in second[0]])

    def pass_first_0():
        arrive(first[0])
        start(onward[0])
        core[2].start()
        arrive((gate_a, gate_b))
        start((gate_c3, gate_c5, gate_d))

    def pass_first_1():
        arrive(first[1])
        start(onward[1])
        core[3].start()
        start([pieces[1] for pieces in second[0]])
        start([pieces[0] for pieces in second[1]])

    def pass_diagonal_0():
        arrive(onward[0])
        core[4].start()
        gate_d.wait_recv()
        gate_c7.start()

    def pass_diagonal_1():
        arrive(onward[1])
        core[5].start()

    def pass_second(i):
        for pieces in second[i]:
            arrive(pieces)
        core[6 + i].start()

    gate_tiles = {
        0: gsend.at[0], 1: g_c.at[0], 2: g_a.at[0], 3: g_c.at[1],
        4: g_b.at[0], 5: g_c.at[2], 6: g_d.at[0], 7: g_c.at[3],
    }

    def hidden(s, part, e):
        tokens = xs[s, part]
        mask = jnp.concatenate([G[e, part]] * (w1.shape[2] // 128), axis=1) > 0.0
        a = jnp.dot(tokens, w1[e], preferred_element_type=F32)
        b = jnp.dot(tokens, w3[e], preferred_element_type=F32)
        return jnp.where(mask, a * (1.0 / (1.0 + jnp.exp(-a))) * b, 0.0).astype(BF16)

    def experts(s, total, finish, hooks=None, parts=(0, 1)):
        hooks = hooks or {}
        part = pl.ds(parts[0] * half, len(parts) * half)
        left = lax.broadcasted_iota(jnp.int32, (1, half), 1) < QUARTER
        for e in range(local_experts):
            for i in parts:
                (o0, h0, _), (o1, h1, _) = BLOCKS[s][2 * i:2 * i + 2]
                row = gate_tiles[o0][pl.ds(2 * e + h0, 1), :]
                if (o0, h0) != (o1, h1):
                    row = jnp.where(left, row, gate_tiles[o1][pl.ds(2 * e + h1, 1), :])
                G[e, pl.ds(i * half, half), :] = jnp.broadcast_to(row, (half, half)).T
        act = None
        for e in range(local_experts + 1):
            for hook in hooks.get(e, ()):
                hook()
            later = hidden(s, part, e) if e < local_experts else None
            if act is not None:
                out = jnp.dot(act, w2[e - 1], preferred_element_type=F32)
                out = out * jnp.concatenate([G[e - 1, part]] * (w2.shape[2] // 128), axis=1)
                if e == 1:
                    total[part, :] = out
                elif e < local_experts:
                    total[part, :] += out
                else:
                    finish(out)
            act = later

    back_c = {s: remote(out_c.at[s - 2], rec_c.at[s - 2], "C") for s in range(2, 8)}
    back_own = [remote(out_c1.at[part], rec_c1.at[part], "C") for part in (upper, lower)]
    back, through = {}, {}

    def finish_own(out):
        own[...] = own[...] + out

    def finish_core_own(i):
        part = (upper, lower)[i]

        def finish(out):
            out_c1[part, :] = (acc[0, part, :] + out).astype(BF16)
        return finish

    def finish_pair(s):
        def finish(out):
            out_c[s - 2] = (acc[s % 2, upper, :] + out[:half]).astype(BF16)
            acc[s % 2, lower, :] += out[half:]
        return finish

    def send_chip(s):
        i = s - 2
        back_c[s].wait_recv()
        for j, (owner, h, q) in enumerate(BLOCKS[s][2:]):
            part = pl.ds(j * QUARTER, QUARTER)
            total = acc[s % 2, pl.ds(half + j * QUARTER, QUARTER), :] + rec_c[i, part, :].astype(F32)
            if (owner, h) in ((2, 1), (4, 0)):
                through[6, h, q].wait_recv()
                total = total + (d_b if owner == 2 else d_a)[q].astype(F32)
            pb[i, part, :] = total.astype(BF16)
            row = pl.ds(token_row(h, q), QUARTER)
            if owner == 6:
                to, dst = ("A", d_a.at[q]) if h == 0 else ("B", d_b.at[q])
                through[6, h, q] = copy = remote(pb.at[i, part], dst, to)
            else:
                to, dst = ("A", r_a.at[row]) if owner == 2 else ("B", r_b.at[row])
                back[owner, h, q] = copy = remote(pb.at[i, part], dst, to)
            copy.start()

    def pair(s, hooks):
        core[s].wait_recv()
        experts(s, acc.at[s % 2], finish_pair(s), hooks)
        back_c[s].start()

    def await_weights(e):
        for copy in load_w[e - 1][2:] + load_w[e][:2]:
            copy.wait()

    do = functools.partial
    experts(0, own, finish_own, {e: [do(await_weights, e)] for e in range(local_experts + 1)})
    pass_first_0()
    arrive((core_own, gate_c))
    experts(1, acc.at[0], finish_core_own(0), parts=(0,))
    back_own[0].start()
    arrive((gate_c3, gate_c5))
    pair(2, {2: [pass_first_1]})
    pair(3, {3: [do(send_chip, 2), pass_diagonal_0]})
    gate_c7.wait_recv()
    pair(4, {3: [do(send_chip, 3), pass_diagonal_1]})
    pair(5, {3: [do(send_chip, 4), do(pass_second, 0), do(pass_second, 1)]})
    pair(6, {3: [do(send_chip, 5)]})
    pair(7, {3: [do(send_chip, 6)]})
    experts(1, acc.at[0], finish_core_own(1), {3: [do(send_chip, 7)]}, parts=(1,))
    back_own[1].start()

    arrive(back_own)
    own[...] = own[...] + rec_c1[...].astype(F32) + xs[0].astype(F32)
    for q in range(2):
        row_0, row_1 = pl.ds(token_row(0, q), QUARTER), pl.ds(token_row(1, q), QUARTER)
        arrive((back[2, 0, q], back[4, 1, q]))
        own[row_0, :] = own[row_0, :] + r_a[row_0, :].astype(F32)
        own[row_1, :] = own[row_1, :] + r_b[row_1, :].astype(F32)
    stores = []
    for s in (6, 7):
        for owner, h, q in BLOCKS[s][2:]:
            row = pl.ds(token_row(h, q), QUARTER)
            back[owner, h, q].wait_recv()
            y_buf[row, :] = (own[row, :] + (r_a if owner == 2 else r_b)[row, :].astype(F32)).astype(BF16)
            stores.append(local(y_buf.at[row], y_hbm.at[row]))
            stores[-1].start()
    for copy in stores:
        copy.wait()
    for copy in sent:
        copy.wait_send()


def solution(mesh):
    axes = tuple(mesh.axis_names)
    row_spec, w_spec = P(axes, None), P(axes, None, None)

    def local_layer(tokens, expert_ids, gate_weights, w_gate, w_up, w_down):
        rows, width = tokens.shape
        experts, _, ff = w_gate.shape
        top_k = expert_ids.shape[1]
        return pl.pallas_call(
            moe_kernel,
            name="moe_layer",
            out_shape=jax.ShapeDtypeStruct((rows, width), BF16),
            in_specs=[pl.BlockSpec(memory_space=pltpu.HBM)] * 6,
            out_specs=pl.BlockSpec(memory_space=pltpu.HBM),
            scratch_shapes=[
                pltpu.VMEM((8, rows, width), BF16),
                pltpu.VMEM((experts, width, ff), BF16),
                pltpu.VMEM((experts, width, ff), BF16),
                pltpu.VMEM((experts, ff, width), BF16),
                pltpu.VMEM((top_k, rows), jnp.int32),
                pltpu.VMEM((top_k, rows), F32),
                pltpu.VMEM((8, 8, 128), F32),
                pltpu.VMEM((4, 8, 128), F32),
                pltpu.VMEM((2, 8, 128), F32),
                pltpu.VMEM((2, 8, 128), F32),
                pltpu.VMEM((4, 8, 128), F32),
                pltpu.VMEM((experts, rows, 128), F32),
                pltpu.VMEM((2, rows, width), F32),
                pltpu.VMEM((rows, width), F32),
                pltpu.VMEM((rows, width), BF16),
                pltpu.VMEM((rows, width), BF16),
                pltpu.VMEM((6, rows // 2, width), BF16),
                pltpu.VMEM((6, rows // 2, width), BF16),
                pltpu.VMEM((6, rows // 2, width), BF16),
                pltpu.VMEM((rows, width), BF16),
                pltpu.VMEM((rows, width), BF16),
                pltpu.VMEM((2, QUARTER, width), BF16),
                pltpu.VMEM((2, QUARTER, width), BF16),
                pltpu.VMEM((rows, width), BF16),
                pltpu.SemaphoreType.DMA((20,)),
                pltpu.SemaphoreType.DMA((48,)),
                pltpu.SemaphoreType.DMA((48,)),
            ],
            compiler_params=pltpu.CompilerParams(
                collective_id=0, has_side_effects=True, vmem_limit_bytes=60 * 2**20
            ),
        )(tokens, expert_ids.T, gate_weights.T, w_gate, w_up, w_down)

    return jax.shard_map(
        local_layer, mesh=mesh,
        in_specs=(row_spec, row_spec, row_spec, w_spec, w_spec, w_spec),
        out_specs=row_spec, check_vma=False,
    )
```

time: 201 us -> 44.3 us (0.22)
  local copies, waits for them, and re-layouts: 79.4 us -> 1.87 us
  blocking collectives: 51.7 us -> 0 us
  Pallas kernels: 0 us -> 42.3 us
  other arithmetic: 33.2 us -> 0 us
  matrix products: 28.4 us -> 0 us
  starting transfers between devices: 7.58 us -> 0 us
    all_to_all x1 -> x0, blocking collectives: 51.7 us -> none  [local_layer(): returned = lax.all_to_all(back_rows, ep_axes, 0, 0, tiled=True)]
    pallas_call x0 -> x1, Pallas kernels: none -> 42.3 us  [local_layer(): pl.pallas_call(moe_kernel, name='moe_layer', out_shape=jax.ShapeDtypeStru...]
    another operation x3 -> x0, local copies, waits for them, and re-layouts: 30.8 us -> none  [the longest x1 30.6 us: local_layer(): jax.ops.segment_sum(weighted.reshape(-1, hidden), pick_rows.reshape(-1),...]
    unnamed x11 -> x1, local copies, waits for them, and re-layouts: 31.5 us -> 1.87 us
    dot_general x4 -> x0, matrix products: 28.4 us -> none  [the longest x1 13.7 us: expert_ffn(): jnp.einsum('lcf,lfh->lch', hidden_act, w_down, preferred_element_type=jnp...]
    scatter-add x1 -> x0, other arithmetic: 22.7 us -> none  [local_layer(): jax.ops.segment_sum(weighted.reshape(-1, hidden), pick_rows.reshape(-1),...]
    gather x1 -> x0, local copies, waits for them, and re-layouts: 13.7 us -> none  [local_layer(): flat_rows[pick_rows]]
    all_to_all x2 -> x0, starting transfers between devices: 7.58 us -> none  [the longest x1 4.3 us: local_layer(): recv_gates = lax.all_to_all(send_gates, ep_axes, 0, 0, tiled=True)]
  transfers between devices with their start and end apart: 2 -> 0, of which waited for: 1 -> 0; matrix products, arithmetic and copies ran while one was open for 35% -> 0% of each run, Pallas kernels for 0% -> 0%
where the time goes in v2:
time: 44.3 us; the launch traced here: 44.1 us
  Pallas kernels  42.3 us (95%)
  local copies, waits for them, and re-layouts  1.87 us (4%)
    pallas_call x1, Pallas kernels, local_layer(): pl.pallas_call(moe_kernel, name='moe_layer', out_shape=jax.ShapeDtypeStru...  42.3 us
    unnamed x1, local copies, waits for them, and re-layouts  1.87 us

profile of v2, /device:TPU:0, one launch (start us, length us, event | category | flops | bytes accessed | tf_op | source)
XLA Modules:
  0.0 44.1 jit_solution(8488131421832293156)
XLA Ops:
  0.0 42.3 %moe_layer.1 = bf16[256,1024]{1,0:T(8,128)(2,1)} custom-call(bf16[256,1024]{1,0:T(8,128)(2,1)} %x_hbm.1, s32[8,256]{1,0:T(8,128)} %bitcast.2, f32[8,256]{1,0:T(8,128)} %bitcast.3, bf16[4,1024,512]{2,1,0:T(8,128)(2,1)} %w1_hbm.1, bf16[4,1024,512]{2,1,0:T(8,128)(2,1)} %w3_hbm.1, bf16[4,512,1024]{2,1,0:T(8,128)(2,1)} %w2_hbm.1), custom_call_target="tpu_custom_call" | custom-call | tf_op jit(solution)/shard_map/moe_layer/pallas_call | solution.py:290
  42.3 1.9 %copy.8 = bf16[256,1024]{1,0:T(8,128)(2,1)} copy(bf16[256,1024]{1,0:T(8,128)(2,1)} %moe_layer.1) | data formatting | bytes 1048576

commit v3 on v2

--- a/solution.py
+++ b/solution.py
@@ -35,31 +35,28 @@
 
 
 def moe_kernel(
-    x_hbm, ids_hbm, gates_hbm, w1_hbm, w3_hbm, w2_hbm, y_hbm,
+    x_hbm, ids_hbm, gates_hbm, w1_hbm, w3_hbm, w2_hbm, y_ref,
     xs, w1, w3, w2, ids, gates, gsend, g_a, g_b, g_d, g_c, G,
-    acc, own, out_c1, rec_c1, out_c, rec_c, pb, r_a, r_b, d_a, d_b, y_buf, lsem, ssem, rsem,
+    acc, own, out_c1, rec_c1, out_c, rec_c, pb, r_a, r_b, d_ab, lsem, ssem, rsem,
 ):
     z, y, x = lax.axis_index("ez"), lax.axis_index("ey"), lax.axis_index("ex")
     me = 4 * z + 2 * y + x
     dev = {"A": (z, 1 - y, x), "B": (1 - z, y, x), "C": (z, y, 1 - x)}
     half = 2 * QUARTER
     local_experts = w1.shape[0]
-    count = [0, 0]
-    sent = []
-
-    def local(src, dst):
-        copy = pltpu.make_async_copy(src, dst, lsem.at[count[0]])
-        count[0] += 1
-        return copy
-
-    def remote(src, dst, to):
-        copy = pltpu.make_async_remote_copy(
-            src_ref=src, dst_ref=dst, send_sem=ssem.at[count[1]], recv_sem=rsem.at[count[1]],
+    names = {}
+
+    def await_all(sem, like):
+        pltpu.make_async_copy(like, like, sem).wait()
+
+    def received(name):
+        return rsem.at[names.setdefault(name, len(names))]
+
+    def remote(src, dst, to, name, kind=0):
+        return pltpu.make_async_remote_copy(
+            src_ref=src, dst_ref=dst, send_sem=ssem.at[kind], recv_sem=received(name),
             device_id=dev[to], device_id_type=MESH,
         )
-        count[1] += 1
-        sent.append(copy)
-        return copy
 
     def rows(piece, skip=0, size=QUARTER):
         s, row = place(piece)
@@ -69,18 +66,23 @@
         for copy in copies:
             copy.start()
 
-    def arrive(copies):
-        for copy in copies:
-            copy.wait_recv()
-
-    load_x = local(x_hbm, xs.at[0])
-    load_ids, load_gates = local(ids_hbm, ids), local(gates_hbm, gates)
-    start((load_x, load_ids, load_gates))
-    load_w = []
+    def arrive(name, like):
+        await_all(received(name), like)
+
+    def load(src, dst, sem):
+        pltpu.make_async_copy(src, dst, lsem.at[sem]).start()
+
+    load(x_hbm, xs.at[0], 0)
+    load(ids_hbm, ids, 1)
+    load(gates_hbm, gates, 1)
     for e in range(local_experts):
-        load_w.append([local(s.at[e], d.at[e]) for s, d in ((w1_hbm, w1), (w3_hbm, w3), (w2_hbm, w2))])
-        start(load_w[e])
-    load_w.append([])
+        load(w1_hbm.at[e], w1.at[e], 2 + e)
+        load(w3_hbm.at[e], w3.at[e], 2 + e)
+        load(w2_hbm.at[e], w2.at[e], 3 + e)
+
+    def await_weights(e):
+        matrices = 2 * (e < local_experts) + (e > 0)
+        await_all(lsem.at[2 + e], w1.at[pl.ds(0, matrices)])
 
     barrier = pltpu.get_barrier_semaphore()
     for to in "ABC":
@@ -88,32 +90,31 @@
 
     first, second, onward = ([], []), ([], []), ([], [])
     for i in range(2):
-        s1, s2, s3 = 2 + i, 4 + i, 6 + i
+        s1, s3 = 2 + i, 6 + i
         for owner, h, q in BLOCKS[s1][2:]:
             to, across = ("A", "B") if owner == 2 else ("B", "A")
-            first[i].append(remote(rows((0, h, q)), rows((owner, h, q)), to))
-            onward[i].append(remote(rows((owner, h, q)), rows((6, h, q)), across))
+            first[i].append(remote(rows((0, h, q)), rows((owner, h, q)), to, ("first", i)))
+            onward[i].append(remote(rows((owner, h, q)), rows((6, h, q)), across, ("onward", i)))
         for owner, h, q in BLOCKS[s3][2:]:
             to = "A" if owner == 2 else "B"
             cuts = ((0, 32), (32, 32)) if i == 0 else ((0, QUARTER),)
-            second[i].append([remote(rows((0, h, q), *cut), rows((owner, h, q), *cut), to) for cut in cuts])
-    core_own = remote(xs.at[0], xs.at[1], "C")
+            second[i].append([remote(rows((0, h, q), *cut), rows((owner, h, q), *cut), to, ("second", i)) for cut in cuts])
+    core_own = remote(xs.at[0], xs.at[1], "C", "core_own")
     upper, lower = pl.ds(0, half), pl.ds(half, half)
-    core = {s: remote(xs.at[s, lower], xs.at[s, upper], "C") for s in range(2, 8)}
-    gate_a = remote(gsend.at[pl.ds(4, 4)], g_a, "A")
-    gate_b = remote(gsend.at[pl.ds(2, 2)], g_b, "B")
-    gate_c = remote(gsend.at[pl.ds(1, 1)], g_c.at[pl.ds(0, 1)], "C")
-    gate_d = remote(g_a.at[pl.ds(2, 2)], g_d, "B")
-    gate_c3 = remote(g_a.at[pl.ds(1, 1)], g_c.at[pl.ds(1, 1)], "C")
-    gate_c5 = remote(g_b.at[pl.ds(1, 1)], g_c.at[pl.ds(2, 1)], "C")
-    gate_c7 = remote(g_d.at[pl.ds(1, 1)], g_c.at[pl.ds(3, 1)], "C")
-
-    load_x.wait()
+    core = {s: remote(xs.at[s, lower], xs.at[s, upper], "C", ("core", s)) for s in range(2, 8)}
+    gate_a = remote(gsend.at[pl.ds(4, 4)], g_a, "A", "gate_ab", 2)
+    gate_b = remote(gsend.at[pl.ds(2, 2)], g_b, "B", "gate_ab", 2)
+    gate_c = remote(gsend.at[pl.ds(1, 1)], g_c.at[pl.ds(0, 1)], "C", "gate_c", 2)
+    gate_d = remote(g_a.at[pl.ds(2, 2)], g_d, "B", "gate_d", 2)
+    gate_c3 = remote(g_a.at[pl.ds(1, 1)], g_c.at[pl.ds(1, 1)], "C", "gate_c35", 2)
+    gate_c5 = remote(g_b.at[pl.ds(1, 1)], g_c.at[pl.ds(2, 1)], "C", "gate_c35", 2)
+    gate_c7 = remote(g_d.at[pl.ds(1, 1)], g_c.at[pl.ds(3, 1)], "C", "gate_c7", 2)
+
+    await_all(lsem.at[0], xs.at[0])
     pl.semaphore_wait(barrier, 3)
     start(first[0])
 
-    load_ids.wait()
-    load_gates.wait()
+    await_all(lsem.at[1], gsend.at[pl.ds(0, 4)])
     ids_v, gates_v = ids[...], gates[...]
     for p, k in enumerate(GATE_ORDER):
         base = (me ^ k) * local_experts
@@ -126,32 +127,31 @@
     start([pieces[0] for pieces in second[0]])
 
     def pass_first_0():
-        arrive(first[0])
+        arrive(("first", 0), xs.at[2, lower])
         start(onward[0])
         core[2].start()
-        arrive((gate_a, gate_b))
+        arrive("gate_ab", gsend.at[pl.ds(0, 6)])
         start((gate_c3, gate_c5, gate_d))
 
     def pass_first_1():
-        arrive(first[1])
+        arrive(("first", 1), xs.at[3, lower])
         start(onward[1])
         core[3].start()
         start([pieces[1] for pieces in second[0]])
         start([pieces[0] for pieces in second[1]])
 
     def pass_diagonal_0():
-        arrive(onward[0])
+        arrive(("onward", 0), xs.at[4, lower])
         core[4].start()
-        gate_d.wait_recv()
+        arrive("gate_d", g_d)
         gate_c7.start()
 
     def pass_diagonal_1():
-        arrive(onward[1])
+        arrive(("onward", 1), xs.at[5, lower])
         core[5].start()
 
     def pass_second(i):
-        for pieces in second[i]:
-            arrive(pieces)
+        arrive(("second", i), xs.at[6 + i, lower])
         core[6 + i].start()
 
     gate_tiles = {
@@ -193,9 +193,8 @@
                     finish(out)
             act = later
 
-    back_c = {s: remote(out_c.at[s - 2], rec_c.at[s - 2], "C") for s in range(2, 8)}
-    back_own = [remote(out_c1.at[part], rec_c1.at[part], "C") for part in (upper, lower)]
-    back, through = {}, {}
+    back_c = {s: remote(out_c.at[s - 2], rec_c.at[s - 2], "C", ("back_c", s), 1) for s in range(2, 8)}
+    back_own = [remote(out_c1.at[part], rec_c1.at[part], "C", "back_own", 1) for part in (upper, lower)]
 
     def finish_own(out):
         own[...] = own[...] + out
@@ -215,68 +214,60 @@
 
     def send_chip(s):
         i = s - 2
-        back_c[s].wait_recv()
+        arrive(("back_c", s), rec_c.at[i])
+        if s >= 6:
+            arrive(("through", s - 2), d_ab.at[s - 6])
         for j, (owner, h, q) in enumerate(BLOCKS[s][2:]):
             part = pl.ds(j * QUARTER, QUARTER)
             total = acc[s % 2, pl.ds(half + j * QUARTER, QUARTER), :] + rec_c[i, part, :].astype(F32)
-            if (owner, h) in ((2, 1), (4, 0)):
-                through[6, h, q].wait_recv()
-                total = total + (d_b if owner == 2 else d_a)[q].astype(F32)
+            if s >= 6:
+                total = total + d_ab[s - 6, 1 if owner == 2 else 0].astype(F32)
             pb[i, part, :] = total.astype(BF16)
             row = pl.ds(token_row(h, q), QUARTER)
             if owner == 6:
-                to, dst = ("A", d_a.at[q]) if h == 0 else ("B", d_b.at[q])
-                through[6, h, q] = copy = remote(pb.at[i, part], dst, to)
+                copy = remote(pb.at[i, part], d_ab.at[s - 4, h], "A" if h == 0 else "B", ("through", s), 1)
             else:
+                name = ("back", s) if s >= 6 else "back"
                 to, dst = ("A", r_a.at[row]) if owner == 2 else ("B", r_b.at[row])
-                back[owner, h, q] = copy = remote(pb.at[i, part], dst, to)
+                copy = remote(pb.at[i, part], dst, to, name, 1)
             copy.start()
 
     def pair(s, hooks):
-        core[s].wait_recv()
+        arrive(("core", s), xs.at[s, upper])
         experts(s, acc.at[s % 2], finish_pair(s), hooks)
         back_c[s].start()
-
-    def await_weights(e):
-        for copy in load_w[e - 1][2:] + load_w[e][:2]:
-            copy.wait()
 
     do = functools.partial
     experts(0, own, finish_own, {e: [do(await_weights, e)] for e in range(local_experts + 1)})
     pass_first_0()
-    arrive((core_own, gate_c))
+    arrive("core_own", xs.at[1])
+    arrive("gate_c", g_c.at[pl.ds(0, 1)])
     experts(1, acc.at[0], finish_core_own(0), parts=(0,))
     back_own[0].start()
-    arrive((gate_c3, gate_c5))
+    arrive("gate_c35", g_c.at[pl.ds(1, 2)])
     pair(2, {2: [pass_first_1]})
     pair(3, {3: [do(send_chip, 2), pass_diagonal_0]})
-    gate_c7.wait_recv()
+    arrive("gate_c7", g_c.at[pl.ds(3, 1)])
     pair(4, {3: [do(send_chip, 3), pass_diagonal_1]})
     pair(5, {3: [do(send_chip, 4), do(pass_second, 0), do(pass_second, 1)]})
     pair(6, {3: [do(send_chip, 5)]})
-    pair(7, {3: [do(send_chip, 6)]})
-    experts(1, acc.at[0], finish_core_own(1), {3: [do(send_chip, 7)]}, parts=(1,))
+    pair(7, {2: [do(send_chip, 6)]})
+    experts(1, acc.at[0], finish_core_own(1), {2: [do(send_chip, 7)]}, parts=(1,))
     back_own[1].start()
 
-    arrive(back_own)
+    arrive("back_own", rec_c1)
     own[...] = own[...] + rec_c1[...].astype(F32) + xs[0].astype(F32)
-    for q in range(2):
-        row_0, row_1 = pl.ds(token_row(0, q), QUARTER), pl.ds(token_row(1, q), QUARTER)
-        arrive((back[2, 0, q], back[4, 1, q]))
-        own[row_0, :] = own[row_0, :] + r_a[row_0, :].astype(F32)
-        own[row_1, :] = own[row_1, :] + r_b[row_1, :].astype(F32)
-    stores = []
+    arrive("back", r_a)
+    own[upper, :] = own[upper, :] + r_a[upper, :].astype(F32)
+    own[lower, :] = own[lower, :] + r_b[lower, :].astype(F32)
     for s in (6, 7):
+        arrive(("back", s), r_a.at[upper])
         for owner, h, q in BLOCKS[s][2:]:
             row = pl.ds(token_row(h, q), QUARTER)
-            back[owner, h, q].wait_recv()
-            y_buf[row, :] = (own[row, :] + (r_a if owner == 2 else r_b)[row, :].astype(F32)).astype(BF16)
-            stores.append(local(y_buf.at[row], y_hbm.at[row]))
-            stores[-1].start()
-    for copy in stores:
-        copy.wait()
-    for copy in sent:
-        copy.wait_send()
+            y_ref[row, :] = (own[row, :] + (r_a if owner == 2 else r_b)[row, :].astype(F32)).astype(BF16)
+    await_all(ssem.at[0], xs.at[pl.ds(0, 7)])
+    await_all(ssem.at[1], xs.at[pl.ds(0, 7)])
+    await_all(ssem.at[2], G.at[0, pl.ds(0, 96)])
 
 
 def solution(mesh):
@@ -292,7 +283,7 @@
             name="moe_layer",
             out_shape=jax.ShapeDtypeStruct((rows, width), BF16),
             in_specs=[pl.BlockSpec(memory_space=pltpu.HBM)] * 6,
-            out_specs=pl.BlockSpec(memory_space=pltpu.HBM),
+            out_specs=pl.BlockSpec(memory_space=pltpu.VMEM),
             scratch_shapes=[
                 pltpu.VMEM((8, rows, width), BF16),
                 pltpu.VMEM((experts, width, ff), BF16),
@@ -315,17 +306,15 @@
                 pltpu.VMEM((6, rows // 2, width), BF16),
                 pltpu.VMEM((rows, width), BF16),
                 pltpu.VMEM((rows, width), BF16),
-                pltpu.VMEM((2, QUARTER, width), BF16),
-                pltpu.VMEM((2, QUARTER, width), BF16),
-                pltpu.VMEM((rows, width), BF16),
-                pltpu.SemaphoreType.DMA((20,)),
-                pltpu.SemaphoreType.DMA((48,)),
-                pltpu.SemaphoreType.DMA((48,)),
+                pltpu.VMEM((2, 2, QUARTER, width), BF16),
+                pltpu.SemaphoreType.DMA((7,)),
+                pltpu.SemaphoreType.DMA((3,)),
+                pltpu.SemaphoreType.DMA((30,)),
             ],
             compiler_params=pltpu.CompilerParams(
-                collective_id=0, has_side_effects=True, vmem_limit_bytes=60 * 2**20
+                collective_id=0, has_side_effects=True, vmem_limit_bytes=46 * 2**20
             ),
-        )(tokens, expert_ids.T, gate_weights.T, w_gate, w_up, w_down)
+        )(*(pltpu.with_memory_space_constraint(v, pltpu.HBM) for v in (tokens, expert_ids.T, gate_weights.T, w_gate, w_up, w_down)))
 
     return jax.shard_map(
         local_layer, mesh=mesh,

time: 44.3 us -> 41.6 us (0.939)
  Pallas kernels: 42.3 us -> 40.7 us
  local copies, waits for them, and re-layouts: 1.87 us -> 0.8 us
    pallas_call x1, Pallas kernels: 42.3 us -> 40.7 us  [local_layer(): pl.pallas_call(moe_kernel, name='moe_layer', out_shape=jax.ShapeDtypeStru...]
    unnamed x1, local copies, waits for them, and re-layouts: 1.87 us -> 0.8 us
where the time goes in v3:
time: 41.6 us; the launch traced here: 41.5 us
  Pallas kernels  40.7 us (98%)
  local copies, waits for them, and re-layouts  0.8 us (2%)
    pallas_call x1, Pallas kernels, local_layer(): pl.pallas_call(moe_kernel, name='moe_layer', out_shape=jax.ShapeDtypeStru...  40.7 us

profile of v3, /device:TPU:0, one launch (start us, length us, event | category | flops | bytes accessed | tf_op | source)
XLA Modules:
  0.0 41.5 jit_solution(15973688293957062959)
XLA Ops:
  0.0 40.7 %moe_layer.1 = bf16[256,1024]{1,0:T(8,128)(2,1)S(1)} custom-call(bf16[256,1024]{1,0:T(8,128)(2,1)} %x_hbm.1, s32[8,256]{1,0:T(8,128)} %bitcast.2, f32[8,256]{1,0:T(8,128)} %bitcast.3, bf16[4,1024,512]{2,1,0:T(8,128)(2,1)} %w1_hbm.1, bf16[4,1024,512]{2,1,0:T(8,128)(2,1)} %w3_hbm.1, bf16[4,512,1024]{2,1,0:T(8,128)(2,1)} %w2_hbm.1), custom_call_target="tpu_custom_call" | custom-call | tf_op jit(solution)/shard_map/moe_layer/pallas_call | solution.py:281
  40.7 0.8 %copy.8 = bf16[256,1024]{1,0:T(8,128)(2,1)} copy(bf16[256,1024]{1,0:T(8,128)(2,1)S(1)} %moe_layer.1) | data formatting | bytes 1048576

commit v4 on v3

--- a/solution.py
+++ b/solution.py
@@ -72,9 +72,9 @@
     def load(src, dst, sem):
         pltpu.make_async_copy(src, dst, lsem.at[sem]).start()
 
-    load(x_hbm, xs.at[0], 0)
     load(ids_hbm, ids, 1)
     load(gates_hbm, gates, 1)
+    load(x_hbm, xs.at[0], 0)
     for e in range(local_experts):
         load(w1_hbm.at[e], w1.at[e], 2 + e)
         load(w3_hbm.at[e], w3.at[e], 2 + e)
@@ -98,10 +98,10 @@
         for owner, h, q in BLOCKS[s3][2:]:
             to = "A" if owner == 2 else "B"
             cuts = ((0, 32), (32, 32)) if i == 0 else ((0, QUARTER),)
-            second[i].append([remote(rows((0, h, q), *cut), rows((owner, h, q), *cut), to, ("second", i)) for cut in cuts])
+            second[i].append([remote(rows((0, h, q), *cut), rows((owner, h, q), *cut), to, "second") for cut in cuts])
     core_own = remote(xs.at[0], xs.at[1], "C", "core_own")
     upper, lower = pl.ds(0, half), pl.ds(half, half)
-    core = {s: remote(xs.at[s, lower], xs.at[s, upper], "C", ("core", s)) for s in range(2, 8)}
+    core = {s: remote(xs.at[s, lower], xs.at[s, upper], "C", ("core", min(s, 6))) for s in range(2, 8)}
     gate_a = remote(gsend.at[pl.ds(4, 4)], g_a, "A", "gate_ab", 2)
     gate_b = remote(gsend.at[pl.ds(2, 2)], g_b, "B", "gate_ab", 2)
     gate_c = remote(gsend.at[pl.ds(1, 1)], g_c.at[pl.ds(0, 1)], "C", "gate_c", 2)
@@ -109,10 +109,6 @@
     gate_c3 = remote(g_a.at[pl.ds(1, 1)], g_c.at[pl.ds(1, 1)], "C", "gate_c35", 2)
     gate_c5 = remote(g_b.at[pl.ds(1, 1)], g_c.at[pl.ds(2, 1)], "C", "gate_c35", 2)
     gate_c7 = remote(g_d.at[pl.ds(1, 1)], g_c.at[pl.ds(3, 1)], "C", "gate_c7", 2)
-
-    await_all(lsem.at[0], xs.at[0])
-    pl.semaphore_wait(barrier, 3)
-    start(first[0])
 
     await_all(lsem.at[1], gsend.at[pl.ds(0, 4)])
     ids_v, gates_v = ids[...], gates[...]
@@ -122,8 +118,12 @@
             row = jnp.sum(jnp.where(ids_v == base + e, gates_v, 0.0), axis=0, keepdims=True)
             gsend[p, pl.ds(2 * e, 1), :] = row[:, :half]
             gsend[p, pl.ds(2 * e + 1, 1), :] = row[:, half:]
-    start((gate_a, gate_b, gate_c, core_own))
+    await_all(lsem.at[0], xs.at[0])
+    pl.semaphore_wait(barrier, 3)
+    start(first[0])
+    start((gate_a, gate_b))
     start(first[1])
+    start((gate_c, core_own))
     start([pieces[0] for pieces in second[0]])
 
     def pass_first_0():
@@ -150,9 +150,9 @@
         arrive(("onward", 1), xs.at[5, lower])
         core[5].start()
 
-    def pass_second(i):
-        arrive(("second", i), xs.at[6 + i, lower])
-        core[6 + i].start()
+    def pass_second():
+        arrive("second", xs.at[pl.ds(6, 2), lower])
+        start((core[6], core[7]))
 
     gate_tiles = {
         0: gsend.at[0], 1: g_c.at[0], 2: g_a.at[0], 3: g_c.at[1],
@@ -199,17 +199,19 @@
     def finish_own(out):
         own[...] = own[...] + out
 
-    def finish_core_own(i):
-        part = (upper, lower)[i]
-
+    def finish_core_own(part):
         def finish(out):
             out_c1[part, :] = (acc[0, part, :] + out).astype(BF16)
         return finish
 
-    def finish_pair(s):
+    def finish_core(s):
         def finish(out):
             out_c[s - 2] = (acc[s % 2, upper, :] + out[:half]).astype(BF16)
-            acc[s % 2, lower, :] += out[half:]
+        return finish
+
+    def finish_chip(s):
+        def finish(out):
+            acc[s % 2, lower, :] += out[-half:]
         return finish
 
     def send_chip(s):
@@ -232,9 +234,13 @@
                 copy = remote(pb.at[i, part], dst, to, name, 1)
             copy.start()
 
-    def pair(s, hooks):
-        arrive(("core", s), xs.at[s, upper])
-        experts(s, acc.at[s % 2], finish_pair(s), hooks)
+    def pair(s, *hooks):
+        def finish(out):
+            finish_core(s)(out)
+            finish_chip(s)(out)
+        if s < 7:
+            arrive(("core", s), xs.at[s, upper] if s < 6 else xs.at[pl.ds(6, 2), upper])
+        experts(s, acc.at[s % 2], finish, {2: hooks})
         back_c[s].start()
 
     do = functools.partial
@@ -242,29 +248,33 @@
     pass_first_0()
     arrive("core_own", xs.at[1])
     arrive("gate_c", g_c.at[pl.ds(0, 1)])
-    experts(1, acc.at[0], finish_core_own(0), parts=(0,))
+    experts(1, acc.at[0], finish_core_own(upper), parts=(0,))
     back_own[0].start()
     arrive("gate_c35", g_c.at[pl.ds(1, 2)])
-    pair(2, {2: [pass_first_1]})
-    pair(3, {3: [do(send_chip, 2), pass_diagonal_0]})
+    pair(2, pass_first_1)
+    pair(3, do(send_chip, 2), pass_diagonal_0)
     arrive("gate_c7", g_c.at[pl.ds(3, 1)])
-    pair(4, {3: [do(send_chip, 3), pass_diagonal_1]})
-    pair(5, {3: [do(send_chip, 4), do(pass_second, 0), do(pass_second, 1)]})
-    pair(6, {3: [do(send_chip, 5)]})
-    pair(7, {2: [do(send_chip, 6)]})
-    experts(1, acc.at[0], finish_core_own(1), {2: [do(send_chip, 7)]}, parts=(1,))
+    pair(4, do(send_chip, 3), pass_diagonal_1)
+    pair(5, do(send_chip, 4), pass_second)
+    pair(6, do(send_chip, 5))
+    experts(7, acc.at[1], finish_core(7), {3: [do(send_chip, 6)]}, parts=(0,))
+    back_c[7].start()
+    experts(7, acc.at[1], finish_chip(7), parts=(1,))
+    send_chip(7)
+    experts(1, acc.at[0], finish_core_own(lower), parts=(1,))
     back_own[1].start()
 
-    arrive("back_own", rec_c1)
-    own[...] = own[...] + rec_c1[...].astype(F32) + xs[0].astype(F32)
+    own[...] = own[...] + xs[0].astype(F32)
     arrive("back", r_a)
     own[upper, :] = own[upper, :] + r_a[upper, :].astype(F32)
     own[lower, :] = own[lower, :] + r_b[lower, :].astype(F32)
+    arrive("back_own", rec_c1)
     for s in (6, 7):
         arrive(("back", s), r_a.at[upper])
         for owner, h, q in BLOCKS[s][2:]:
             row = pl.ds(token_row(h, q), QUARTER)
-            y_ref[row, :] = (own[row, :] + (r_a if owner == 2 else r_b)[row, :].astype(F32)).astype(BF16)
+            last = (r_a if owner == 2 else r_b)[row, :].astype(F32)
+            y_ref[row, :] = (own[row, :] + rec_c1[row, :].astype(F32) + last).astype(BF16)
     await_all(ssem.at[0], xs.at[pl.ds(0, 7)])
     await_all(ssem.at[1], xs.at[pl.ds(0, 7)])
     await_all(ssem.at[2], G.at[0, pl.ds(0, 96)])
@@ -309,7 +319,7 @@
                 pltpu.VMEM((2, 2, QUARTER, width), BF16),
                 pltpu.SemaphoreType.DMA((7,)),
                 pltpu.SemaphoreType.DMA((3,)),
-                pltpu.SemaphoreType.DMA((30,)),
+                pltpu.SemaphoreType.DMA((28,)),
             ],
             compiler_params=pltpu.CompilerParams(
                 collective_id=0, has_side_effects=True, vmem_limit_bytes=46 * 2**20

time: 41.6 us -> 40.9 us (0.983)
  Pallas kernels: 40.7 us -> 40 us
    pallas_call x1, Pallas kernels: 40.7 us -> 40 us  [local_layer(): pl.pallas_call(moe_kernel, name='moe_layer', out_shape=jax.ShapeDtypeStru...]
where the time goes in v4:
time: 40.9 us; the launch traced here: 40.8 us
  Pallas kernels  40 us (98%)
  local copies, waits for them, and re-layouts  0.8 us (2%)
    pallas_call x1, Pallas kernels, local_layer(): pl.pallas_call(moe_kernel, name='moe_layer', out_shape=jax.ShapeDtypeStru...  40 us

profile of v4, /device:TPU:0, one launch (start us, length us, event | category | flops | bytes accessed | tf_op | source)
XLA Modules:
  0.0 40.8 jit_solution(13661518383524613327)
XLA Ops:
  0.0 40.0 %moe_layer.1 = bf16[256,1024]{1,0:T(8,128)(2,1)S(1)} custom-call(bf16[256,1024]{1,0:T(8,128)(2,1)} %x_hbm.1, s32[8,256]{1,0:T(8,128)} %bitcast.2, f32[8,256]{1,0:T(8,128)} %bitcast.3, bf16[4,1024,512]{2,1,0:T(8,128)(2,1)} %w1_hbm.1, bf16[4,1024,512]{2,1,0:T(8,128)(2,1)} %w3_hbm.1, bf16[4,512,1024]{2,1,0:T(8,128)(2,1)} %w2_hbm.1), custom_call_target="tpu_custom_call" | custom-call | tf_op jit(solution)/shard_map/moe_layer/pallas_call | solution.py:291
  40.0 0.8 %copy.8 = bf16[256,1024]{1,0:T(8,128)(2,1)} copy(bf16[256,1024]{1,0:T(8,128)(2,1)S(1)} %moe_layer.1) | data formatting | bytes 1048576

commit v5 on v4

--- a/solution.py
+++ b/solution.py
@@ -214,6 +214,8 @@
             acc[s % 2, lower, :] += out[-half:]
         return finish
 
+    held = []
+
     def send_chip(s):
         i = s - 2
         arrive(("back_c", s), rec_c.at[i])
@@ -228,11 +230,20 @@
             row = pl.ds(token_row(h, q), QUARTER)
             if owner == 6:
                 copy = remote(pb.at[i, part], d_ab.at[s - 4, h], "A" if h == 0 else "B", ("through", s), 1)
+            elif s == 3:
+                to, dst = ("A", r_a) if owner == 2 else ("B", r_b)
+                rest, copy = (
+                    remote(pb.at[i, pl.ds(j * QUARTER + skip, 32)], dst.at[pl.ds(token_row(h, q) + skip, 32)], to, "back", 1)
+                    for skip in (32, 0)
+                )
+                held.append(rest)
             else:
                 name = ("back", s) if s >= 6 else "back"
                 to, dst = ("A", r_a.at[row]) if owner == 2 else ("B", r_b.at[row])
                 copy = remote(pb.at[i, part], dst, to, name, 1)
             copy.start()
+        if s == 4:
+            start(held)
 
     def pair(s, *hooks):
         def finish(out):
@@ -260,8 +271,8 @@
     experts(7, acc.at[1], finish_core(7), {3: [do(send_chip, 6)]}, parts=(0,))
     back_c[7].start()
     experts(7, acc.at[1], finish_chip(7), parts=(1,))
-    send_chip(7)
-    experts(1, acc.at[0], finish_core_own(lower), parts=(1,))
+    pl.when(x == 0)(do(send_chip, 7))
+    experts(1, acc.at[0], finish_core_own(lower), {3: [do(pl.when(x == 1), do(send_chip, 7))]}, parts=(1,))
     back_own[1].start()
 
     own[...] = own[...] + xs[0].astype(F32)

time: 40.9 us -> 40.6 us (level)
  no operation moved by 1% of the time
where the time goes in v5:
time: 40.6 us; the launch traced here: 40.5 us
  Pallas kernels  39.6 us (98%)
  local copies, waits for them, and re-layouts  0.8 us (2%)
    pallas_call x1, Pallas kernels, local_layer(): pl.pallas_call(moe_kernel, name='moe_layer', out_shape=jax.ShapeDtypeStru...  39.6 us

profile of v5, /device:TPU:0, one launch (start us, length us, event | category | flops | bytes accessed | tf_op | source)
XLA Modules:
  0.0 40.5 jit_solution(1035450199673879378)
XLA Ops:
  0.0 39.6 %moe_layer.1 = bf16[256,1024]{1,0:T(8,128)(2,1)S(1)} custom-call(bf16[256,1024]{1,0:T(8,128)(2,1)} %x_hbm.1, s32[8,256]{1,0:T(8,128)} %bitcast.2, f32[8,256]{1,0:T(8,128)} %bitcast.3, bf16[4,1024,512]{2,1,0:T(8,128)(2,1)} %w1_hbm.1, bf16[4,1024,512]{2,1,0:T(8,128)(2,1)} %w3_hbm.1, bf16[4,512,1024]{2,1,0:T(8,128)(2,1)} %w2_hbm.1), custom_call_target="tpu_custom_call" | custom-call | tf_op jit(solution)/shard_map/moe_layer/pallas_call | solution.py:302
  39.7 0.8 %copy.8 = bf16[256,1024]{1,0:T(8,128)(2,1)} copy(bf16[256,1024]{1,0:T(8,128)(2,1)S(1)} %moe_layer.1) | data formatting | bytes 1048576

commit v6 on v5

--- a/solution.py
+++ b/solution.py
@@ -72,9 +72,9 @@
     def load(src, dst, sem):
         pltpu.make_async_copy(src, dst, lsem.at[sem]).start()
 
+    load(x_hbm, xs.at[0], 0)
     load(ids_hbm, ids, 1)
     load(gates_hbm, gates, 1)
-    load(x_hbm, xs.at[0], 0)
     for e in range(local_experts):
         load(w1_hbm.at[e], w1.at[e], 2 + e)
         load(w3_hbm.at[e], w3.at[e], 2 + e)
@@ -166,9 +166,9 @@
         b = jnp.dot(tokens, w3[e], preferred_element_type=F32)
         return jnp.where(mask, a * (1.0 / (1.0 + jnp.exp(-a))) * b, 0.0).astype(BF16)
 
-    def experts(s, total, finish, hooks=None, parts=(0, 1)):
+    def experts(s, total, finish, hooks=None, parts=(0, 1), part=None):
         hooks = hooks or {}
-        part = pl.ds(parts[0] * half, len(parts) * half)
+        part = part or pl.ds(parts[0] * half, len(parts) * half)
         left = lax.broadcasted_iota(jnp.int32, (1, half), 1) < QUARTER
         for e in range(local_experts):
             for i in parts:
@@ -202,16 +202,6 @@
     def finish_core_own(part):
         def finish(out):
             out_c1[part, :] = (acc[0, part, :] + out).astype(BF16)
-        return finish
-
-    def finish_core(s):
-        def finish(out):
-            out_c[s - 2] = (acc[s % 2, upper, :] + out[:half]).astype(BF16)
-        return finish
-
-    def finish_chip(s):
-        def finish(out):
-            acc[s % 2, lower, :] += out[-half:]
         return finish
 
     held = []
@@ -247,10 +237,9 @@
 
     def pair(s, *hooks):
         def finish(out):
-            finish_core(s)(out)
-            finish_chip(s)(out)
-        if s < 7:
-            arrive(("core", s), xs.at[s, upper] if s < 6 else xs.at[pl.ds(6, 2), upper])
+            out_c[s - 2] = (acc[s % 2, upper, :] + out[:half]).astype(BF16)
+            acc[s % 2, lower, :] += out[half:]
+        arrive(("core", s), xs.at[s, upper] if s < 6 else xs.at[pl.ds(6, 2), upper])
         experts(s, acc.at[s % 2], finish, {2: hooks})
         back_c[s].start()
 
@@ -268,11 +257,22 @@
     pair(4, do(send_chip, 3), pass_diagonal_1)
     pair(5, do(send_chip, 4), pass_second)
     pair(6, do(send_chip, 5))
-    experts(7, acc.at[1], finish_core(7), {3: [do(send_chip, 6)]}, parts=(0,))
-    back_c[7].start()
-    experts(7, acc.at[1], finish_chip(7), parts=(1,))
-    pl.when(x == 0)(do(send_chip, 7))
-    experts(1, acc.at[0], finish_core_own(lower), {3: [do(pl.when(x == 1), do(send_chip, 7))]}, parts=(1,))
+    near, far = (pl.ds(pl.multiple_of(i * half, half), half) for i in (1 - x, x))
+
+    def finish_half(part):
+        def finish(out):
+            acc[1, part, :] += out
+        return finish
+
+    def exchange():
+        out_c[5] = acc[1, upper, :].astype(BF16)
+        back_c[7].start()
+
+    experts(7, acc.at[1], finish_half(near), {3: [do(send_chip, 6)]}, part=near)
+    pl.when(x == 1)(exchange)
+    experts(7, acc.at[1], finish_half(far), {3: [do(pl.when(x == 0), do(send_chip, 7))]}, parts=(), part=far)
+    pl.when(x == 0)(exchange)
+    experts(1, acc.at[0], finish_core_own(lower), {2: [do(pl.when(x == 1), do(send_chip, 7))]}, parts=(1,))
     back_own[1].start()
 
     own[...] = own[...] + xs[0].astype(F32)

time: 40.6 us -> 40.6 us (level); the launches traced: 40.5 us -> 40 us
    pallas_call x1, Pallas kernels: 39.6 us -> 39.2 us  [local_layer(): pl.pallas_call(moe_kernel, name='moe_layer', out_shape=jax.ShapeDtypeStru...]
where the time goes in v6:
time: 40.6 us; the launch traced here: 40 us
  Pallas kernels  39.2 us (97%)
  local copies, waits for them, and re-layouts  0.8 us (2%)
    pallas_call x1, Pallas kernels, local_layer(): pl.pallas_call(moe_kernel, name='moe_layer', out_shape=jax.ShapeDtypeStru...  39.2 us

profile of v6, /device:TPU:0, one launch (start us, length us, event | category | flops | bytes accessed | tf_op | source)
XLA Modules:
  0.0 40.0 jit_solution(7342102806014449)
XLA Ops:
  0.0 39.2 %moe_layer.1 = bf16[256,1024]{1,0:T(8,128)(2,1)S(1)} custom-call(bf16[256,1024]{1,0:T(8,128)(2,1)} %x_hbm.1, s32[8,256]{1,0:T(8,128)} %bitcast.2, f32[8,256]{1,0:T(8,128)} %bitcast.3, bf16[4,1024,512]{2,1,0:T(8,128)(2,1)} %w1_hbm.1, bf16[4,1024,512]{2,1,0:T(8,128)(2,1)} %w3_hbm.1, bf16[4,512,1024]{2,1,0:T(8,128)(2,1)} %w2_hbm.1), custom_call_target="tpu_custom_call" | custom-call | tf_op jit(solution)/shard_map/moe_layer/pallas_call | solution.py:302
  39.2 0.8 %copy.8 = bf16[256,1024]{1,0:T(8,128)(2,1)} copy(bf16[256,1024]{1,0:T(8,128)(2,1)S(1)} %moe_layer.1) | data formatting | bytes 1048576

commit v7 on v5

--- a/solution.py
+++ b/solution.py
@@ -72,16 +72,16 @@
     def load(src, dst, sem):
         pltpu.make_async_copy(src, dst, lsem.at[sem]).start()
 
+    load(x_hbm, xs.at[0], 0)
     load(ids_hbm, ids, 1)
     load(gates_hbm, gates, 1)
-    load(x_hbm, xs.at[0], 0)
     for e in range(local_experts):
         load(w1_hbm.at[e], w1.at[e], 2 + e)
         load(w3_hbm.at[e], w3.at[e], 2 + e)
-        load(w2_hbm.at[e], w2.at[e], 3 + e)
+        load(w2_hbm.at[e], w2.at[e], 2 + min(e + 1, local_experts - 1))
 
     def await_weights(e):
-        matrices = 2 * (e < local_experts) + (e > 0)
+        matrices = 2 + (e > 0) + (e == local_experts - 1)
         await_all(lsem.at[2 + e], w1.at[pl.ds(0, matrices)])
 
     barrier = pltpu.get_barrier_semaphore()
@@ -255,7 +255,7 @@
         back_c[s].start()
 
     do = functools.partial
-    experts(0, own, finish_own, {e: [do(await_weights, e)] for e in range(local_experts + 1)})
+    experts(0, own, finish_own, {e: [do(await_weights, e)] for e in range(local_experts)})
     pass_first_0()
     arrive("core_own", xs.at[1])
     arrive("gate_c", g_c.at[pl.ds(0, 1)])
@@ -328,7 +328,7 @@
                 pltpu.VMEM((rows, width), BF16),
                 pltpu.VMEM((rows, width), BF16),
                 pltpu.VMEM((2, 2, QUARTER, width), BF16),
-                pltpu.SemaphoreType.DMA((7,)),
+                pltpu.SemaphoreType.DMA((6,)),
                 pltpu.SemaphoreType.DMA((3,)),
                 pltpu.SemaphoreType.DMA((28,)),
             ],

time: 40.6 us -> 40.5 us (level)
  no operation moved by 1% of the time
where the time goes in v7:
time: 40.5 us; the launch traced here: 40.4 us
  Pallas kernels  39.6 us (98%)
  local copies, waits for them, and re-layouts  0.8 us (2%)
    pallas_call x1, Pallas kernels, local_layer(): pl.pallas_call(moe_kernel, name='moe_layer', out_shape=jax.ShapeDtypeStru...  39.6 us

profile of v7, /device:TPU:0, one launch (start us, length us, event | category | flops | bytes accessed | tf_op | source)
XLA Modules:
  0.0 40.4 jit_solution(17962637972804885536)
XLA Ops:
  0.0 39.6 %moe_layer.1 = bf16[256,1024]{1,0:T(8,128)(2,1)S(1)} custom-call(bf16[256,1024]{1,0:T(8,128)(2,1)} %x_hbm.1, s32[8,256]{1,0:T(8,128)} %bitcast.2, f32[8,256]{1,0:T(8,128)} %bitcast.3, bf16[4,1024,512]{2,1,0:T(8,128)(2,1)} %w1_hbm.1, bf16[4,1024,512]{2,1,0:T(8,128)(2,1)} %w3_hbm.1, bf16[4,512,1024]{2,1,0:T(8,128)(2,1)} %w2_hbm.1), custom_call_target="tpu_custom_call" | custom-call | tf_op jit(solution)/shard_map/moe_layer/pallas_call | solution.py:302
  39.6 0.8 %copy.8 = bf16[256,1024]{1,0:T(8,128)(2,1)} copy(bf16[256,1024]{1,0:T(8,128)(2,1)S(1)} %moe_layer.1) | data formatting | bytes 1048576
